TPU v7x, 32 devices: a whole 2x2x4 slice. The times are simulated.
32 devices in a mesh: grp: 4 (over x, core), seq: 8 (over z, y).
Axes of the slice: x: 2, y: 2, z: 4, core: 2. Of those that a mesh axis runs over, the one named last changes fastest.
Arguments:
- patches: bfloat16 [2048, 1280], P(('grp', 'seq')), may hold values from -60 to 60
- piece_ids: int32 [32, 64], P(('grp', 'seq')), may hold values from 0 to 2, never falling along the last dimension, each value on 1 to 48 neighbouring positions
- vit_gain: float32 [1280], replicated, may hold values from 0.25 to 1.75
- vit_qkv: bfloat16 [1280, 3840], replicated
- vit_out: bfloat16 [1280, 1280], replicated, may hold values from -0.15625 to 0.15625
- merge_gain: float32 [1280], replicated, may hold values from 0.25 to 1.75
- merge_up: bfloat16 [5120, 5120], P(None, 'seq'), may hold values from -0.078125 to 0.078125
- merge_down: bfloat16 [5120, 8192], P(None, 'seq'), may hold values from -0.078125 to 0.078125
- dest: int32 [512], P(('grp', 'seq')), may hold values from 0 to 7, as said below
- tokens: bfloat16 [8192, 8192], P(('grp', 'seq')), may hold values from -60 to 60
- image_index: int32 [8192], P(('grp', 'seq')), may hold values from 0 to 32, as said below
- doc_lengths: int32 [4, 4], P('grp'), may hold values from 1 to 1024, 2048 in all within a row
- attn_gain: float32 [8192], replicated, may hold values from 0.25 to 1.75
- attn_qkv: bfloat16 [8192, 768], P(('grp', 'seq'))
- attn_out: bfloat16 [512, 8192], P(None, ('grp', 'seq')), may hold values from -0.25 to 0.25
Outputs:
- layer_out: bfloat16 [8192, 8192], P(('grp', 'seq'))
Inputs may be any that keep to these rules, and one draw needn't show every extreme that they name: `dest`: within each aligned block of 16 rows (one device's merged rows), exactly 4 distinct values occur, each exactly 4 times, and in every group one device is named by every device of the group. `image_index`: 32 marks a text token. A value k < 32 on a device names the merged row that the device of seq index k // 4 in its group sends to it as its (k % 4)-th row in row order; each such row is named by exactly one token of the receiving device, and no other values occur. `piece_ids`: piece numbers never fall within a window. `doc_lengths`: each group's documents fill its 2048 positions.
All inputs are finite; a program needn't handle non-finite values.
Results may differ from a plain program's by a relative error of at most 0.0093.
The roundings to bfloat16 on the way count: a program that leaves them out, or rounds other values in their place, can miss the bound.
Values may be sent and summed in bfloat16 or wider, within the bound.
A program may use at most 192 MiB of HBM per device.

v0:
```python
import functools

import jax
import jax.numpy as jnp
from jax import lax
from jax.experimental import pallas as pl
from jax.experimental.pallas import tpu as pltpu
from jax.sharding import PartitionSpec as P

VHEADS = 16
WIN = 64
LANES = 128
EPSILON = 1e-06
MESH = pl.DeviceIdType.MESH


def rms_scale(inputs, gain):
    mean_square = jnp.mean(inputs * inputs, axis=-1, keepdims=True)
    return inputs * lax.rsqrt(mean_square + EPSILON) * gain


def slot_numbers(targets):
    row_count = targets.shape[-1]
    order = jnp.arange(row_count, dtype=jnp.int32)
    same = targets[..., :, None] == targets[..., None, :]
    earlier = order[None, :] < order[:, None]
    return jnp.sum(same & earlier, axis=-1)


def greet(n_seq, pairs):
    grp, seq = lax.axis_index("grp"), lax.axis_index("seq")
    barrier = pltpu.get_barrier_semaphore()
    for k in range(1, n_seq):
        pl.semaphore_signal(
            barrier, inc=1, device_id=(grp, lax.rem(seq + k, n_seq)), device_id_type=MESH
        )
    for other in pairs:
        pl.semaphore_signal(barrier, inc=1, device_id=(other, seq), device_id_type=MESH)
    pl.semaphore_wait(barrier, n_seq - 1 + len(pairs))


def flip(index, bit):
    return index + bit - 2 * bit * lax.rem(index // bit, 2)


class Relay:
    def __init__(self, n_seq, shard, full, local_sem, recv_sem, send_sem):
        self.n_seq, self.shard, self.full = n_seq, shard, full
        self.local_sem, self.recv_sem, self.send_sem = local_sem, recv_sem, send_sem
        self.line = n_seq // 2
        self.grp, self.seq = lax.axis_index("grp"), lax.axis_index("seq")
        self.core = lax.rem(self.grp, 2)
        self.place, self.side = self.seq // 2, lax.rem(self.seq, 2)
        far = flip(self.grp, 2)
        self.far = far
        across = flip(self.seq, 1)
        first = self.core == 0
        self.a_dev = (jnp.where(first, far, self.grp), jnp.where(first, self.seq, across))
        self.b_dev = (jnp.where(first, self.grp, far), jnp.where(first, across, self.seq))
        self.ab_dev = (far, across)
        self.core_dev = (flip(self.grp, 1), self.seq)

    def slot(self, base, place):
        return base[0] * self.n_seq + 2 * place + lax.rem(base[1], 2)

    def copy(self, slot, way, device, own=False):
        return pltpu.make_async_remote_copy(
            src_ref=self.shard if own else self.full.at[slot],
            dst_ref=self.full.at[slot],
            send_sem=self.send_sem.at[way, slot],
            recv_sem=self.recv_sem.at[slot],
            device_id=device,
            device_id_type=MESH,
        )

    def up(self):
        return (self.grp, jnp.minimum(self.seq + 2, self.n_seq - 2 + self.side))

    def down(self):
        return (self.grp, jnp.maximum(self.seq - 2, self.side))

    def me(self):
        return (self.grp, self.seq)

    def begin(self):
        slot = self.slot(self.me(), self.place)
        pltpu.make_async_copy(self.shard, self.full.at[slot], self.local_sem).start()

        @pl.when(self.place + 1 < self.line)
        def _():
            self.copy(slot, 0, self.up(), True).start()

        @pl.when(self.place > 0)
        def _():
            self.copy(slot, 1, self.down(), True).start()

        self.copy(slot, 2, self.a_dev, True).start()
        self.copy(slot, 3, self.b_dev, True).start()
        self.copy(slot, 4, self.core_dev, True).start()

    def spots(self, distance):
        low, high = self.place - distance, self.place + distance
        if distance == 0:
            return [(self.place, None, None)]
        return [(low, low >= 0, True), (high, high < self.line, False)]

    def visit(self, base, distance, ways, finish=False):
        for place, there, upward in self.spots(distance):

            def act(place=place, upward=upward):
                slot = self.slot(base, place)
                own_core = base is not None
                if not finish:
                    self.copy(slot, 4, self.core_dev).wait_recv()
                for way, device in ways:
                    move = self.copy(slot, way, device)
                    move.wait_send() if finish else move.start()
                if upward is True and "z" in self.mode:

                    @pl.when(self.place + 1 < self.line)
                    def _():
                        move = self.copy(slot, 0, self.up())
                        move.wait_send() if finish else move.start()

                if upward is False and "z" in self.mode:

                    @pl.when(self.place > 0)
                    def _():
                        move = self.copy(slot, 1, self.down())
                        move.wait_send() if finish else move.start()

            if there is None:
                act()
            else:
                pl.when(there)(act)

    def own_line(self, distance, finish=False):
        self.mode = "z"
        self.visit(
            self.me(), distance,
            [(2, self.a_dev), (3, self.b_dev), (4, self.core_dev)], finish,
        )

    def a_line(self, distance, finish=False):
        self.mode = ""
        self.visit(self.a_dev, distance, [(3, self.b_dev), (4, self.core_dev)], finish)

    def b_lines(self, distance, finish=False):
        self.mode = ""
        self.visit(self.b_dev, distance, [(4, self.core_dev)], finish)
        self.visit(self.ab_dev, distance, [(4, self.core_dev)], finish)

    def step(self, distance):
        if 0 < distance < self.line:
            self.own_line(distance)
        if 0 <= distance - 1 < self.line:
            self.a_line(distance - 1)
        if 0 <= distance - 2 < self.line:
            self.b_lines(distance - 2)

    def steps(self):
        return self.line + 2

    def end(self):
        slot = self.slot(self.me(), self.place)
        pltpu.make_async_copy(self.shard, self.full.at[slot], self.local_sem).wait()

        @pl.when(self.place + 1 < self.line)
        def _():
            self.copy(slot, 0, self.up(), True).wait_send()

        @pl.when(self.place > 0)
        def _():
            self.copy(slot, 1, self.down(), True).wait_send()

        self.copy(slot, 2, self.a_dev, True).wait_send()
        self.copy(slot, 3, self.b_dev, True).wait_send()
        self.copy(slot, 4, self.core_dev, True).wait_send()
        for distance in range(self.line):
            if distance:
                self.own_line(distance, True)
            self.a_line(distance, True)
            self.b_lines(distance, True)
        partner = self.core_dev[0]
        for place in range(self.line):
            for base in (
                (partner, self.seq), (partner, flip(self.seq, 1)),
                (flip(partner, 2), self.seq), (flip(partner, 2), flip(self.seq, 1)),
            ):
                slot = self.slot(base, place)
                self.copy(slot, 4, self.core_dev).wait_recv()


def relay_scratch(n_dev):
    return [
        pltpu.SemaphoreType.DMA,
        pltpu.SemaphoreType.DMA((n_dev,)),
        pltpu.SemaphoreType.DMA((5, n_dev)),
    ]


def swap(n_seq, send_of, land_of, send_sem, recv_sem):
    grp, seq = lax.axis_index("grp"), lax.axis_index("seq")
    moves = []
    for k in range(1, n_seq):
        to = lax.rem(seq + k, n_seq)
        moves.append(
            pltpu.make_async_remote_copy(
                src_ref=send_of(to),
                dst_ref=land_of(seq),
                send_sem=send_sem.at[k],
                recv_sem=recv_sem.at[k],
                device_id=(grp, to),
                device_id_type=MESH,
            )
        )
    for move in moves:
        move.start()
    return moves


def vision_kernel(
    n_seq, slots,
    patches, piece_col, piece_row, vit_gain, vit_qkv, vit_out, merge_gain, merge_up, merge_down,
    code, want, row_base, attn_qkv,
    table, qkv_all,
    up_v, down_v, normed_s, gathered, hidden, stage, landed,
    load_sem, send1, recv1, send2, recv2, send3, recv3, *relay_sems,
):
    seq = lax.axis_index("seq")
    grp = lax.axis_index("grp")
    up_copy = pltpu.make_async_copy(merge_up, up_v, load_sem.at[0])
    down_copy = pltpu.make_async_copy(merge_down, down_v, load_sem.at[1])
    up_copy.start()
    down_copy.start()
    greet(n_seq, (flip(grp, 1), flip(grp, 2)))
    relay = Relay(n_seq, attn_qkv, qkv_all, *relay_sems)
    relay.begin()

    rows, features = patches.shape
    head_dim = features // VHEADS
    residual = patches[...].astype(jnp.float32)
    normed = rms_scale(residual, vit_gain[...]).astype(jnp.bfloat16)
    projected = jnp.dot(normed, vit_qkv[...], preferred_element_type=jnp.float32)
    q = projected[:, :features].astype(jnp.bfloat16).astype(jnp.float32)
    keys = projected[:, features : 2 * features].astype(jnp.bfloat16)
    values = projected[:, 2 * features :].astype(jnp.bfloat16)
    lane = lax.broadcasted_iota(jnp.int32, (rows, features), 1)
    inside = [(lane >= h * head_dim) & (lane < (h + 1) * head_dim) for h in range(VHEADS)]
    stacked = jnp.concatenate(
        [jnp.where(inside[h], q, 0.0).astype(jnp.bfloat16) for h in range(VHEADS)], axis=0
    )
    scores = lax.dot_general(
        stacked, keys, (((1,), (1,)), ((), ())), preferred_element_type=jnp.float32
    ) * head_dim ** (-0.5)
    scores = scores.reshape(VHEADS, rows, rows)
    allowed = piece_col[...] == piece_row[...]
    scores = jnp.where(allowed[None], scores, -1e30)
    weights = jnp.exp(scores - jnp.max(scores, axis=-1, keepdims=True))
    totals = jnp.sum(weights, axis=-1, keepdims=True)
    mixed = jnp.dot(
        weights.reshape(VHEADS * rows, rows).astype(jnp.bfloat16), values,
        preferred_element_type=jnp.float32,
    )
    top = jnp.zeros((rows, features), jnp.float32)
    low = jnp.ones((rows, features), jnp.float32)
    for h in range(VHEADS):
        top = jnp.where(inside[h], mixed[h * rows : (h + 1) * rows], top)
        low = jnp.where(inside[h], totals[h], low)
    mixture = (top / low).astype(jnp.bfloat16)
    residual = residual + jnp.dot(mixture, vit_out[...], preferred_element_type=jnp.float32)
    merged_in = rms_scale(residual, merge_gain[...])
    own = rows // 4
    chunks = features // LANES
    for j in range(chunks):
        normed_s[j] = merged_in[:, j * LANES : (j + 1) * LANES]
    for part in range(4):
        for j in range(chunks):
            start = part * features + j * LANES
            gathered[seq, :, start : start + LANES] = normed_s[
                j, pl.ds(part, own, stride=4), :
            ].astype(jnp.bfloat16)
    gathered[seq, :, 4 * features :] = code[...]
    moves1 = swap(n_seq, lambda to: gathered.at[seq], lambda me: gathered.at[me], send1, recv1)
    relay.step(1)
    up_copy.wait()
    for move in moves1:
        move.wait_recv()
    all_rows = n_seq * own
    entry = gathered[:, :, : 4 * features].reshape(all_rows, 4 * features)
    pre = jnp.dot(entry, up_v[...], preferred_element_type=jnp.float32)
    hidden[seq] = (0.5 * pre * (1.0 + lax.erf(pre * 0.5**0.5))).astype(jnp.bfloat16)
    moves2 = swap(n_seq, lambda to: hidden.at[seq], lambda me: hidden.at[me], send2, recv2)
    relay.step(2)
    down_copy.wait()
    part_width = hidden.shape[2]

    def term(source):
        start = pl.multiple_of(source * part_width, 32)
        return jnp.dot(
            hidden[source], down_v[pl.ds(start, part_width), :], preferred_element_type=jnp.float32
        )

    codes = gathered[:, :, 4 * features :].reshape(all_rows, LANES).astype(jnp.float32)[:, :1]
    select = jnp.where(codes + row_base[...] == want[...], 1.0, 0.0)
    select = jnp.transpose(select).astype(jnp.bfloat16)
    total = term(seq)
    for k in range(1, n_seq):
        moves2[k - 1].wait_recv()
        total = total + term(lax.rem(seq - k + n_seq, n_seq))
    outgoing = jnp.dot(
        select, total.astype(jnp.bfloat16), preferred_element_type=jnp.float32
    ).astype(jnp.bfloat16)
    stage[...] = outgoing.reshape(stage.shape)
    landed[seq] = stage[seq]
    moves3 = swap(n_seq, lambda to: stage.at[to], lambda me: landed.at[me], send3, recv3)
    for distance in range(3, relay.steps()):
        relay.step(distance)
    for move in moves3:
        move.wait_recv()
    width = landed.shape[2]
    for source in range(n_seq):
        table[:, source * width : (source + 1) * width] = landed[source]
    for moves in (moves1, moves2, moves3):
        for move in moves:
            move.wait_send()
    relay.end()


def attend_kernel(
    n_seq, reach, heads,
    queries, own_kv, positions, starts, attn_out,
    attended, out_all,
    kv, load_sem, send_sem, recv_sem, *relay_sems,
):
    grp, seq = lax.axis_index("grp"), lax.axis_index("seq")
    rows, width = own_kv.shape
    head_dim = width // 2
    greet(n_seq, (flip(grp, 1), flip(grp, 2)))
    moves = []
    for k in range(1, reach + 1):
        moves.append(
            pltpu.make_async_remote_copy(
                src_ref=own_kv,
                dst_ref=kv.at[reach - k],
                send_sem=send_sem.at[k],
                recv_sem=recv_sem.at[k],
                device_id=(grp, lax.rem(seq + k, n_seq)),
                device_id_type=MESH,
            )
        )
    for move in moves:
        move.start()
    relay = Relay(n_seq, attn_out, out_all, *relay_sems)
    relay.begin()
    kv[reach] = own_kv[...]
    for move in moves:
        move.wait_recv()
    span = (reach + 1) * rows
    everything = kv[...].reshape(span, width)
    keys, values = everything[:, :head_dim], everything[:, head_dim:]
    key_pos = (seq - reach) * rows + lax.broadcasted_iota(jnp.int32, (rows, span), 1)
    allowed = (key_pos >= starts[...]) & (key_pos <= positions[...])
    for distance in range(relay.steps()):
        relay.step(distance)
        for h in range(heads) if distance == 1 else ():
            scores = lax.dot_general(
                queries[:, h * head_dim : (h + 1) * head_dim], keys,
                (((1,), (1,)), ((), ())), preferred_element_type=jnp.float32,
            ) * head_dim ** (-0.5)
            scores = jnp.where(allowed, scores, -1e30)
            weights = jnp.exp(scores - jnp.max(scores, axis=-1, keepdims=True))
            totals = jnp.sum(weights, axis=-1, keepdims=True)
            mixed = jnp.dot(
                weights.astype(jnp.bfloat16), values, preferred_element_type=jnp.float32
            )
            attended[:, h * head_dim : (h + 1) * head_dim] = (mixed / totals).astype(jnp.bfloat16)
    for move in moves:
        move.wait_send()
    relay.end()


def out_kernel(attended, weight, layer_in, result):
    width = weight.shape[2]
    for i in range(weight.shape[0]):
        columns = slice(i * width, (i + 1) * width)
        update = jnp.dot(attended[...], weight[i], preferred_element_type=jnp.float32)
        result[:, columns] = (layer_in[:, columns].astype(jnp.float32) + update).astype(jnp.bfloat16)


VMEM = pl.BlockSpec(memory_space=pltpu.VMEM)
ANY = pl.BlockSpec(memory_space=pl.ANY)


def on_device(
    patches, piece_ids, vit_gain, vit_qkv, vit_out, merge_gain, merge_up, merge_down, dest,
    tokens, image_index, doc_lengths, attn_gain, attn_qkv, attn_out,
):
    rows, features = patches.shape
    n_seq, n_grp = lax.axis_size("seq"), lax.axis_size("grp")
    n_dev = n_seq * n_grp
    seq_index = lax.axis_index("seq")
    own = rows // 4
    all_rows = n_seq * own
    capacity = own // (n_seq // 2)
    slots = n_seq * capacity
    bf16, f32 = jnp.bfloat16, jnp.float32

    windows = jnp.arange(rows, dtype=jnp.int32) // WIN
    pieces = piece_ids.reshape(-1) + windows * WIN
    code = dest * capacity + slot_numbers(dest).astype(jnp.int32)
    code = jnp.broadcast_to(code[:, None], (own, LANES)).astype(bf16)
    column = jnp.arange(n_seq * slots, dtype=jnp.int32)
    target, place = column // slots, column % slots
    want = (place // capacity) * (n_seq * capacity) + target * capacity + place % capacity
    row_base = (jnp.arange(all_rows, dtype=jnp.int32) // own) * (n_seq * capacity)

    up_width, down_width = merge_up.shape[1], merge_down.shape[1]
    table, qkv_all = pl.pallas_call(
        functools.partial(vision_kernel, n_seq, slots),
        out_shape=(
            jax.ShapeDtypeStruct((slots, n_seq * down_width), bf16),
            jax.ShapeDtypeStruct((n_dev,) + attn_qkv.shape, bf16),
        ),
        in_specs=[VMEM] * 7 + [ANY] * 2 + [VMEM] * 4,
        out_specs=(VMEM, ANY),
        scratch_shapes=[
            pltpu.VMEM(merge_up.shape, bf16),
            pltpu.VMEM(merge_down.shape, bf16),
            pltpu.VMEM((features // LANES, rows, LANES), f32),
            pltpu.VMEM((n_seq, own, 4 * features + LANES), bf16),
            pltpu.VMEM((n_seq, all_rows, up_width), bf16),
            pltpu.VMEM((n_seq, slots, down_width), bf16),
            pltpu.VMEM((n_seq, slots, down_width), bf16),
            pltpu.SemaphoreType.DMA((2,)),
        ] + [pltpu.SemaphoreType.DMA((n_seq,))] * 6 + relay_scratch(n_dev),
        compiler_params=pltpu.CompilerParams(
            collective_id=0, has_side_effects=True, vmem_limit_bytes=66000000
        ),
    )(
        patches, pieces[:, None], pieces[None, :], vit_gain[None], vit_qkv, vit_out,
        merge_gain[None], merge_up, merge_down, code, want.astype(f32)[None],
        row_base.astype(f32)[:, None], attn_qkv,
    )

    slot_all = jnp.arange(slots, dtype=jnp.int32)
    picker = (image_index[:, None] == slot_all[None, :]).astype(bf16)
    pictured = jnp.dot(picker, table, preferred_element_type=f32).astype(bf16)
    layer_in = jnp.where((image_index < slots)[:, None], pictured, tokens)
    tok_rows = tokens.shape[0]
    normed = rms_scale(layer_in.astype(f32), attn_gain).astype(bf16)
    projected = jnp.dot(
        normed, qkv_all.reshape(-1, attn_qkv.shape[1]), preferred_element_type=f32
    ).astype(bf16)
    query_width = attn_out.shape[0]
    queries = projected[:, :query_width]
    key_value = projected[:, query_width:]
    head_dim = key_value.shape[1] // 2
    head_count = query_width // head_dim
    positions = seq_index * tok_rows + jnp.arange(tok_rows, dtype=jnp.int32)
    lengths = doc_lengths[0]
    starts = jnp.cumsum(lengths) - lengths
    doc_start = jnp.max(
        jnp.where(starts[None, :] <= positions[:, None], starts[None, :], 0), axis=1
    )
    reach = n_seq // 2
    attended, out_all = pl.pallas_call(
        functools.partial(attend_kernel, n_seq, reach, head_count),
        out_shape=(
            jax.ShapeDtypeStruct((tok_rows, query_width), bf16),
            jax.ShapeDtypeStruct((n_dev,) + attn_out.shape, bf16),
        ),
        in_specs=[VMEM] * 5,
        out_specs=(VMEM, ANY),
        scratch_shapes=[
            pltpu.VMEM((reach + 1, tok_rows, 2 * head_dim), bf16),
            pltpu.SemaphoreType.DMA((2,)),
            pltpu.SemaphoreType.DMA((reach + 1,)),
            pltpu.SemaphoreType.DMA((reach + 1,)),
        ] + relay_scratch(n_dev),
        compiler_params=pltpu.CompilerParams(
            collective_id=1, has_side_effects=True, vmem_limit_bytes=60000000
        ),
    )(queries, key_value, positions[:, None], doc_start[:, None], attn_out)

    step = n_dev // 8
    wide = step * attn_out.shape[1]
    return pl.pallas_call(
        out_kernel,
        grid=(n_dev // step,),
        out_shape=jax.ShapeDtypeStruct(tokens.shape, bf16),
        in_specs=[
            pl.BlockSpec((tok_rows, query_width), lambda i: (0, 0)),
            pl.BlockSpec((step,) + attn_out.shape, lambda i: (i, 0, 0)),
            pl.BlockSpec((tok_rows, wide), lambda i: (0, i)),
        ],
        out_specs=pl.BlockSpec((tok_rows, wide), lambda i: (0, i)),
    )(attended, out_all, layer_in)


def solution(mesh):
    placed = (
        P(("grp", "seq"), None),
        P(("grp", "seq"), None),
        P(),
        P(),
        P(),
        P(),
        P(None, "seq"),
        P(None, "seq"),
        P(("grp", "seq")),
        P(("grp", "seq"), None),
        P(("grp", "seq")),
        P("grp", None),
        P(),
        P(("grp", "seq"), None),
        P(None, ("grp", "seq")),
    )
    return jax.shard_map(
        on_device, mesh=mesh, in_specs=placed, out_specs=P(("grp", "seq"), None), check_vma=False
    )
```

profile of v0, /device:TPU:25, one launch (start us, length us, event | category | flops | bytes accessed | tf_op | source)
XLA Modules:
  0.0 209.4 jit_solution(8593538267739588378)
XLA Ops:
  0.0 0.7 copy.22
  0.7 0.6 fusion.18.piece_col
  1.4 1.2 fusion.28.piece_row
  2.6 1.3 broadcast_in_dim.23.vit_gain
  3.9 1.3 broadcast_in_dim.24.merge_gain
  5.2 0.9 convert_reduce_fusion
  6.1 0.7 add_convert_fusion
  6.8 0.7 broadcast_in_dim.25.code
  7.4 0.6 fusion.26.want
  8.0 0.6 fusion.12.row_base
  8.7 116.0 %shard_map.145 = (bf16[32,8192]{1,0:T(8,128)(2,1)}, bf16[32,256,768]{2,1,0:T(8,128)(2,1)}) custom-call(bf16[64,1280]{1,0:T(8,128)(2,1)} %patches.1, s32[64,1]{1,0:T(8,128)} %fusion.18.piece_col, s32[1,64]{1,0:T(1,128)} %fusion.28.piece_row, f32[1,1280]{1,0:T(1,128)} %broadcast_in_dim.23.vit_gain, bf16[1280,3840]{1,0:T(8,128)(2,1)} %vit_qkv.1, ...), custom_call_target="tpu_custom_call" | custom-call | tf_op jit(solution)/shard_map/pallas_call | solution.py:419
  124.7 0.0 copy-start.1
  124.7 3.8 %fusion.1 = (f32[256]{0:T(256)S(1)}, bf16[256,8192]{1,0:T(8,128)(2,1)S(1)}) fusion(bf16[256,8192]{1,0:T(8,128)(2,1)} %param.24, bf16[32,8192]{1,0:T(8,128)(2,1)} %get-tuple-element.9, s32[256]{0:T(256)S(1)} %copy-done.2, pred[256]{0:T(512)(128)(4,1)S(1)} %broadcast_compare_fusion), kind=kOutput, calls=%fused_computation.4 | convolution fusion | flops 144711424 | bytes 8915200 | tf_op jit(solution)/shard_map/dot_general | solution.py:448
  128.6 0.0 copy-start.3
  128.6 8.1 %fusion.8 = bf16[256,768]{1,0:T(8,128)(2,1)S(1)} fusion(bf16[8192,768]{1,0:T(8,128)(2,1)} %bitcast.9, bf16[256,8192]{1,0:T(8,128)(2,1)S(1)} %get-tuple-element.14.layer_in, f32[8192]{0:T(1024)S(1)} %copy-done.1, f32[256]{0:T(256)S(1)} %add_rsqrt_fusion), kind=kOutput, calls=%fused_computation.10 | convolution fusion | flops 3229810688 | bytes 17204224 | tf_op jit(solution)/shard_map/dot_general | solution.py:452
  136.7 0.0 copy-done
  136.8 0.7 slice.8.queries
  137.5 0.7 slice.9.own_kv
  138.1 0.7 iota_add_fusion.positions
  138.8 0.2 reduce-window_clone.1
  139.0 0.1 select_reduce_fusion
  139.1 0.8 copy.23.starts
  139.9 59.4 %shard_map.146 = (bf16[256,512]{1,0:T(8,128)(2,1)}, bf16[32,512,256]{2,1,0:T(8,128)(2,1)}) custom-call(bf16[256,512]{1,0:T(8,128)(2,1)} %slice.8.queries, bf16[256,256]{1,0:T(8,128)(2,1)} %slice.9.own_kv, s32[256,1]{1,0:T(8,128)} %iota_add_fusion.positions, s32[256,1]{1,0:T(8,128)} %copy.23.starts, bf16[512,256]{1,0:T(8,128)(2,1)} %attn_out.1), custom_call_target="tpu_custom_call" | custom-call | tf_op jit(solution)/shard_map/pallas_call | solution.py:467
  199.2 10.2 %shard_map.147 = bf16[256,8192]{1,0:T(8,128)(2,1)} custom-call(bf16[256,512]{1,0:T(8,128)(2,1)} %get-tuple-element.11.attended, bf16[32,512,256]{2,1,0:T(8,128)(2,1)} %get-tuple-element.12.weight, bf16[256,8192]{1,0:T(8,128)(2,1)} %copy-done), custom_call_target="tpu_custom_call" | custom-call | tf_op jit(solution)/shard_map/pallas_call | solution.py:488
  (9 shorter events, 0.0 us)
Async XLA Ops:
  8.7 116.0 %copy-start.2 = (s32[256]{0:T(256)S(1)}, s32[256]{0:T(256)}, u32[]{:S(2)}) copy-start(s32[256]{0:T(256)} %param.25) | copy-start | bytes 3076
  124.7 3.9 %copy-start.1 = (f32[8192]{0:T(1024)S(1)}, f32[8192]{0:T(1024)}, u32[]{:S(2)}) copy-start(f32[8192]{0:T(1024)} %param.27) | copy-start | bytes 98308
  128.5 8.2 %copy-start = (bf16[256,8192]{1,0:T(8,128)(2,1)}, bf16[256,8192]{1,0:T(8,128)(2,1)S(1)}, u32[]{:S(2)}) copy-start(bf16[256,8192]{1,0:T(8,128)(2,1)S(1)} %get-tuple-element.14.layer_in) | copy-start | bytes 12582916
  128.6 10.2 %copy-start.3 = (s32[1,4]{1,0:T(1,128)S(1)}, s32[1,4]{1,0:T(1,128)}, u32[]{:S(2)}) copy-start(s32[1,4]{1,0:T(1,128)} %param.26) | copy-start | bytes 52
where the time goes:
time: 214 us; the launch traced here: 209 us
  Pallas kernels  186 us (87%)
  matrix products  12 us (6%)
  local copies, waits for them, and re-layouts  6.19 us (3%)
  other arithmetic  5.6 us (3%)
    pallas_call x1, Pallas kernels, on_device(): pl.pallas_call(functools.partial(vision_kernel, n_seq, slots), out_shape=...  116 us
    pallas_call x1, Pallas kernels, on_device(): pl.pallas_call(functools.partial(attend_kernel, n_seq, reach, head_count)...  59.4 us
    pallas_call x1, Pallas kernels, on_device(): pl.pallas_call(out_kernel, grid=(n_dev // step,), out_shape=jax.ShapeDtyp...  10.2 us
    dot_general x1, matrix products, on_device(): jnp.dot(normed, qkv_all.reshape(-1, attn_qkv.shape[1]), preferred_element...  8.14 us

commit v1 on v0

v1 whole, which is shorter than its diff:
```python
import functools
import math

import jax
import jax.numpy as jnp
from jax import lax
from jax.experimental import pallas as pl
from jax.experimental.pallas import tpu as pltpu
from jax.sharding import PartitionSpec as P

VHEADS = 16
WIN = 64
LANES = 128
EPSILON = 1e-06
AHEAD = 4
MESH = pl.DeviceIdType.MESH


def rms_scale(inputs, gain):
    mean_square = jnp.mean(inputs * inputs, axis=-1, keepdims=True)
    return inputs * lax.rsqrt(mean_square + EPSILON) * gain


def whole_part(values, divisor):
    return jnp.floor((values + 0.5) / divisor)


def greet(n_seq, pairs):
    grp, seq = lax.axis_index("grp"), lax.axis_index("seq")
    barrier = pltpu.get_barrier_semaphore()
    for k in range(1, n_seq):
        pl.semaphore_signal(
            barrier, inc=1, device_id=(grp, lax.rem(seq + k, n_seq)), device_id_type=MESH
        )
    for other in pairs:
        pl.semaphore_signal(barrier, inc=1, device_id=(other, seq), device_id_type=MESH)
    pl.semaphore_wait(barrier, n_seq - 1 + len(pairs))


def flip(index, bit):
    return index + bit - 2 * bit * lax.rem(index // bit, 2)


class Relay:
    def __init__(self, n_seq, shard, full, first, local_sem, recv_sem, send_sem):
        self.n_seq, self.shard, self.full = n_seq, shard, full
        self.local_sem, self.recv_sem, self.send_sem = local_sem, recv_sem, send_sem
        self.line = n_seq // 2
        self.grp, self.seq = lax.axis_index("grp"), lax.axis_index("seq")
        self.place, self.side = self.seq // 2, lax.rem(self.seq, 2)
        far = flip(self.grp, 2)
        self.far = far
        across = flip(self.seq, 1)
        self.a_dev = (jnp.where(first, far, self.grp), jnp.where(first, self.seq, across))
        self.b_dev = (jnp.where(first, self.grp, far), jnp.where(first, across, self.seq))
        self.ab_dev = (far, across)
        self.core_dev = (flip(self.grp, 1), self.seq)

    def slot(self, base, place):
        return base[0] * self.n_seq + 2 * place + lax.rem(base[1], 2)

    def copy(self, slot, way, device, own=False):
        return pltpu.make_async_remote_copy(
            src_ref=self.shard if own else self.full.at[slot],
            dst_ref=self.full.at[slot],
            send_sem=self.send_sem.at[way, slot],
            recv_sem=self.recv_sem.at[slot],
            device_id=device,
            device_id_type=MESH,
        )

    def up(self):
        return (self.grp, jnp.minimum(self.seq + 2, self.n_seq - 2 + self.side))

    def down(self):
        return (self.grp, jnp.maximum(self.seq - 2, self.side))

    def me(self):
        return (self.grp, self.seq)

    def begin(self):
        slot = self.slot(self.me(), self.place)
        pltpu.make_async_copy(self.shard, self.full.at[slot], self.local_sem).start()

        @pl.when(self.place + 1 < self.line)
        def _():
            self.copy(slot, 0, self.up(), True).start()

        @pl.when(self.place > 0)
        def _():
            self.copy(slot, 1, self.down(), True).start()

        self.copy(slot, 2, self.a_dev, True).start()
        self.copy(slot, 3, self.b_dev, True).start()
        self.copy(slot, 4, self.core_dev, True).start()

    def spots(self, distance):
        low, high = self.place - distance, self.place + distance
        if distance == 0:
            return [(self.place, None, None)]
        return [(low, low >= 0, True), (high, high < self.line, False)]

    def visit(self, base, distance, ways, finish=False):
        for place, there, upward in self.spots(distance):

            def act(place=place, upward=upward):
                slot = self.slot(base, place)
                own_core = base is not None
                if not finish:
                    self.copy(slot, 4, self.core_dev).wait_recv()
                for way, device in ways:
                    move = self.copy(slot, way, device)
                    move.wait_send() if finish else move.start()
                if upward is True and "z" in self.mode:

                    @pl.when(self.place + 1 < self.line)
                    def _():
                        move = self.copy(slot, 0, self.up())
                        move.wait_send() if finish else move.start()

                if upward is False and "z" in self.mode:

                    @pl.when(self.place > 0)
                    def _():
                        move = self.copy(slot, 1, self.down())
                        move.wait_send() if finish else move.start()

            if there is None:
                act()
            else:
                pl.when(there)(act)

    def own_line(self, distance, finish=False):
        self.mode = "z"
        self.visit(
            self.me(), distance,
            [(2, self.a_dev), (3, self.b_dev), (4, self.core_dev)], finish,
        )

    def a_line(self, distance, finish=False):
        self.mode = ""
        self.visit(self.a_dev, distance, [(3, self.b_dev), (4, self.core_dev)], finish)

    def b_lines(self, distance, finish=False):
        self.mode = ""
        self.visit(self.b_dev, distance, [(4, self.core_dev)], finish)
        self.visit(self.ab_dev, distance, [(4, self.core_dev)], finish)

    def end(self):
        slot = self.slot(self.me(), self.place)

        @pl.when(self.place + 1 < self.line)
        def _():
            self.copy(slot, 0, self.up(), True).wait_send()

        @pl.when(self.place > 0)
        def _():
            self.copy(slot, 1, self.down(), True).wait_send()

        self.copy(slot, 2, self.a_dev, True).wait_send()
        self.copy(slot, 3, self.b_dev, True).wait_send()
        self.copy(slot, 4, self.core_dev, True).wait_send()
        for distance in range(self.line):
            if distance:
                self.own_line(distance, True)
            self.a_line(distance, True)
            self.b_lines(distance, True)

    def settle(self):
        slot = self.slot(self.me(), self.place)
        pltpu.make_async_copy(self.shard, self.full.at[slot], self.local_sem).wait()
        partner = self.core_dev[0]
        for place in range(self.line):
            for base in (
                (partner, self.seq), (partner, flip(self.seq, 1)),
                (flip(partner, 2), self.seq), (flip(partner, 2), flip(self.seq, 1)),
            ):
                slot = self.slot(base, place)
                self.copy(slot, 4, self.core_dev).wait_recv()


class Gather:
    def __init__(self, n_seq, buf, send_sem, recv_sem):
        self.buf, self.send_sem, self.recv_sem = buf, send_sem, recv_sem
        self.line = n_seq // 2
        self.grp, self.seq = lax.axis_index("grp"), lax.axis_index("seq")
        self.place, self.side = self.seq // 2, lax.rem(self.seq, 2)

    def copy(self, slot, way, place, device):
        return pltpu.make_async_remote_copy(
            src_ref=self.buf.at[slot],
            dst_ref=self.buf.at[slot],
            send_sem=self.send_sem.at[way, place],
            recv_sem=self.recv_sem.at[slot],
            device_id=device,
            device_id_type=MESH,
        )

    def across(self):
        return (self.grp, flip(self.seq, 1))

    def begin(self, finish=False):
        for place in range(self.line):

            @pl.when(self.place != place)
            def _():
                move = self.copy(self.seq, 0, place, (self.grp, 2 * place + self.side))
                move.wait_send() if finish else move.start()

        move = self.copy(self.seq, 1, self.place, self.across())
        move.wait_send() if finish else move.start()

    def forward(self, distance):
        low, high = self.place - distance, self.place + distance
        for place, there in ((low, low >= 0), (high, high < self.line)):

            @pl.when(there)
            def _():
                slot = 2 * place + self.side
                move = self.copy(slot, 1, place, self.across())
                move.wait_recv()
                move.start()

    def settle(self):
        for place in range(self.line):
            slot = 2 * place + 1 - self.side
            self.copy(slot, 1, place, self.across()).wait_recv()

    def end(self):
        self.begin(True)
        for place in range(self.line):

            @pl.when(self.place != place)
            def _():
                slot = 2 * place + self.side
                self.copy(slot, 1, place, self.across()).wait_send()


def relay_scratch(n_dev):
    return [
        pltpu.SemaphoreType.DMA,
        pltpu.SemaphoreType.DMA((n_dev,)),
        pltpu.SemaphoreType.DMA((5, n_dev)),
    ]


def swap(n_seq, send_of, land_of, send_sem, recv_sem):
    grp, seq = lax.axis_index("grp"), lax.axis_index("seq")
    moves = []
    for k in range(1, n_seq):
        to = lax.rem(seq + k, n_seq)
        moves.append(
            pltpu.make_async_remote_copy(
                src_ref=send_of(to),
                dst_ref=land_of(seq),
                send_sem=send_sem.at[k],
                recv_sem=recv_sem.at[k],
                device_id=(grp, to),
                device_id_type=MESH,
            )
        )
    for move in moves:
        move.start()
    return moves


def row_codes(dest, rows, capacity):
    order = lax.broadcasted_iota(jnp.int32, (rows, LANES), 0)
    target = jnp.zeros((rows, LANES), jnp.int32)
    for r in range(rows):
        target = jnp.where(order == r, dest[r], target)
    earlier = jnp.zeros((rows, LANES), jnp.int32)
    for r in range(rows):
        earlier = earlier + jnp.where((target == dest[r]) & (order > r), 1, 0)
    return (target * capacity + earlier).astype(jnp.float32)


def window_attention(projected, pieces, features):
    queries, keys, values = projected
    rows = queries.shape[0]
    head_dim = features // VHEADS
    together = LANES // math.gcd(LANES, head_dim)
    width = together * head_dim
    wide = jnp.broadcast_to(pieces.astype(jnp.float32), (rows, rows))
    allowed = wide == jnp.transpose(wide)
    lane = lax.broadcasted_iota(jnp.int32, (rows, width), 1)
    inside = [(lane >= h * head_dim) & (lane < (h + 1) * head_dim) for h in range(together)]
    parts = []
    for start in range(0, features, width):
        q = queries[:, start : start + width]
        stacked = jnp.concatenate(
            [jnp.where(inside[h], q, 0.0).astype(jnp.bfloat16) for h in range(together)], axis=0
        )
        scores = lax.dot_general(
            stacked, keys[:, start : start + width], (((1,), (1,)), ((), ())),
            preferred_element_type=jnp.float32,
        ) * head_dim ** (-0.5)
        scores = jnp.where(allowed[None], scores.reshape(together, rows, rows), -1e30)
        weights = jnp.exp(scores - jnp.max(scores, axis=-1, keepdims=True))
        totals = jnp.sum(weights, axis=-1, keepdims=True)
        mixed = jnp.dot(
            weights.reshape(together * rows, rows).astype(jnp.bfloat16),
            values[:, start : start + width],
            preferred_element_type=jnp.float32,
        )
        top = jnp.zeros((rows, width), jnp.float32)
        low = jnp.ones((rows, width), jnp.float32)
        for h in range(together):
            top = jnp.where(inside[h], mixed[h * rows : (h + 1) * rows], top)
            low = jnp.where(inside[h], totals[h], low)
        parts.append((top / low).astype(jnp.bfloat16))
    return jnp.concatenate(parts, axis=1)


def layer_kernel(
    n_grp, n_seq, capacity, reach,
    patches, pieces, vit_gain, merge_gain, attn_gain, image_index, dest, doc_lengths,
    vit_qkv, vit_out, merge_up, merge_down, tokens, attn_qkv, attn_out,
    result, out_all,
    wide_v, vit_out_v, up_v, down_v, qkv_all, normed_s, gathered, hidden, stage, landed,
    queries, kv, attended, out_v,
    load_sem, token_sem, result_sem, out_sem, gather_send, hidden_send, gather_recv, hidden_recv,
    table_send, table_recv, kv_send, kv_recv, *relay_sems,
):
    grp, seq = lax.axis_index("grp"), lax.axis_index("seq")
    bf16, f32 = jnp.bfloat16, jnp.float32
    rows, features = patches.shape
    tok_rows = tokens.shape[0]
    slots = n_seq * capacity
    part = features
    vit_loads = [
        pltpu.make_async_copy(
            vit_qkv.at[:, pl.ds(i * part, part)], wide_v.at[:, pl.ds(i * part, part)],
            load_sem.at[i],
        )
        for i in range(3)
    ]
    vit_out_load = pltpu.make_async_copy(vit_out, vit_out_v, load_sem.at[3])
    up_load = pltpu.make_async_copy(merge_up, up_v, load_sem.at[4])
    down_load = pltpu.make_async_copy(merge_down, down_v, load_sem.at[5])
    for load in vit_loads + [vit_out_load]:
        load.start()
    greet(n_seq, (flip(grp, 1), flip(grp, 2)))
    relay = Relay(n_seq, attn_qkv, qkv_all, False, *relay_sems[:3])
    relay.begin()

    chunk_width = merge_down.shape[1]
    per_row = vit_qkv.shape[1] // chunk_width

    def chunk(c):
        return wide_v.at[
            pl.ds((c // per_row) * tok_rows, tok_rows),
            pl.ds((c % per_row) * chunk_width, chunk_width),
        ]

    def chunk_columns(c):
        return pl.ds(c * chunk_width, chunk_width)

    residual = patches[...].astype(f32)
    normed = rms_scale(residual, vit_gain[...].reshape(1, features)).astype(bf16)
    projected = []
    for i in range(3):
        vit_loads[i].wait()
        projected.append(
            jnp.dot(
                normed, wide_v[:, i * part : (i + 1) * part], preferred_element_type=f32
            ).astype(bf16)
        )
    up_load.start()
    down_load.start()
    token_loads = [
        pltpu.make_async_copy(tokens.at[:, chunk_columns(c)], chunk(c), token_sem.at[c])
        for c in range(n_seq)
    ]
    mixture = window_attention(projected, pieces[...], features)
    vit_out_load.wait()
    residual = residual + jnp.dot(mixture, vit_out_v[...], preferred_element_type=f32)
    merged_in = rms_scale(residual, merge_gain[...].reshape(1, features))
    own = rows // 4
    pieces_of = features // LANES
    for j in range(pieces_of):
        normed_s[j] = merged_in[:, j * LANES : (j + 1) * LANES]
    for quarter in range(4):
        for j in range(pieces_of):
            start = quarter * features + j * LANES
            gathered[seq, :, start : start + LANES] = normed_s[
                j, pl.ds(quarter, own, stride=4), :
            ].astype(bf16)
    gathered[seq, :, 4 * features :] = row_codes(dest, own, capacity).astype(bf16)
    first = Gather(n_seq, gathered, gather_send, gather_recv)
    first.begin()
    relay.own_line(1)
    for load in token_loads:
        load.start()
    line = n_seq // 2
    for distance in range(1, line):
        first.forward(distance)
    for distance in range(2, line):
        relay.own_line(distance)
    relay.a_line(0)
    up_load.wait()
    first.settle()

    all_rows = n_seq * own
    entry = gathered[:, :, : 4 * features].reshape(all_rows, 4 * features)
    pre = jnp.dot(entry, up_v[...], preferred_element_type=f32)
    hidden[seq] = (0.5 * pre * (1.0 + lax.erf(pre * 0.5**0.5))).astype(bf16)
    second = Gather(n_seq, hidden, hidden_send, hidden_recv)
    second.begin()

    codes = gathered[:, :, 4 * features :].reshape(all_rows, LANES).astype(f32)[:, :1]
    row = lax.broadcasted_iota(jnp.int32, (all_rows, 1), 0).astype(f32)
    keys = codes + whole_part(row, own) * (n_seq * capacity)
    column = lax.broadcasted_iota(jnp.int32, (1, n_seq * slots), 1).astype(f32)
    target = whole_part(column, slots)
    place = column - target * slots
    source = whole_part(place, capacity)
    want = source * (n_seq * capacity) + target * capacity + place - source * capacity
    select = jnp.transpose(jnp.where(keys == want, 1.0, 0.0)).astype(bf16)

    for distance in range(1, line):
        second.forward(distance)
        relay.a_line(distance)
    down_load.wait()
    part_width = hidden.shape[2]

    def term(index):
        start = pl.multiple_of(index * part_width, 32)
        return jnp.dot(
            hidden[index], down_v[pl.ds(start, part_width), :], preferred_element_type=f32
        )

    side = lax.rem(seq, 2)
    total = term(side)
    for p in range(1, line):
        total = total + term(2 * p + side)
    second.settle()
    for p in range(line):
        total = total + term(2 * p + 1 - side)
    outgoing = jnp.dot(select, total.astype(bf16), preferred_element_type=f32).astype(bf16)
    stage[...] = outgoing.reshape(stage.shape)
    landed[seq] = stage[seq]
    table_moves = swap(
        n_seq, lambda to: stage.at[to], lambda me: landed.at[me], table_send, table_recv
    )
    out_relay = Relay(n_seq, attn_out, out_all, lax.rem(grp, 2) == 0, *relay_sems[3:])
    out_relay.begin()
    for distance in range(line):
        relay.b_lines(distance)

    slot = lax.broadcasted_iota(jnp.int32, (slots, tok_rows), 0)
    picked = jnp.where(slot == image_index[...].reshape(1, tok_rows), 1.0, 0.0)
    picker = jnp.transpose(picked)
    pictured = jnp.sum(picker, axis=1, keepdims=True) > 0.5
    picker = picker.astype(bf16)
    for move in table_moves:
        move.wait_recv()
    square = jnp.zeros((tok_rows, 1), f32)
    for c in range(n_seq):
        token_loads[c].wait()
        image = jnp.dot(picker, landed[c], preferred_element_type=f32)
        layer_in = jnp.where(pictured, image, chunk(c)[...].astype(f32))
        chunk(c)[...] = layer_in.astype(bf16)
        square = square + jnp.sum(layer_in * layer_in, axis=1, keepdims=True)
    out_relay.own_line(1)
    scale = lax.rsqrt(square / (n_seq * chunk_width) + EPSILON)
    relay.settle()
    shard_rows, qkv_width = attn_qkv.shape
    attn_projected = jnp.zeros((tok_rows, qkv_width), f32)
    for c in range(n_seq):
        gain = attn_gain[pl.ds(c * chunk_width, chunk_width)].reshape(1, chunk_width)
        tokens_in = (chunk(c)[...].astype(f32) * scale * gain).astype(bf16)
        weight = qkv_all[c * n_grp : (c + 1) * n_grp].reshape(n_grp * shard_rows, qkv_width)
        attn_projected = attn_projected + jnp.dot(tokens_in, weight, preferred_element_type=f32)
    query_width = attn_out.shape[0]
    queries[...] = attn_projected[:, :query_width].astype(bf16)
    kv[reach] = attn_projected[:, query_width:].astype(bf16)
    kv_moves = []
    for k in range(1, reach + 1):
        kv_moves.append(
            pltpu.make_async_remote_copy(
                src_ref=kv.at[reach],
                dst_ref=kv.at[reach - k],
                send_sem=kv_send.at[k],
                recv_sem=kv_recv.at[k],
                device_id=(grp, lax.rem(seq + k, n_seq)),
                device_id_type=MESH,
            )
        )
        pl.when(seq + k < n_seq)(kv_moves[-1].start)

        @pl.when(seq < k)
        def _():
            kv[reach - k] = jnp.zeros(kv.shape[1:], bf16)

    for distance in range(2, line):
        out_relay.own_line(distance)
    for distance in range(line):
        out_relay.a_line(distance)

    head_dim = kv.shape[2] // 2
    span = (reach + 1) * tok_rows
    position = seq * tok_rows + lax.broadcasted_iota(jnp.int32, (tok_rows, 1), 0)
    begins = jnp.zeros((tok_rows, 1), jnp.int32)
    total_length = jnp.int32(0)
    for k in range(doc_lengths.shape[1]):
        begins = jnp.where(position >= total_length, total_length, begins)
        total_length = total_length + doc_lengths[0, k]
    key_pos = (seq - reach) * tok_rows + lax.broadcasted_iota(jnp.int32, (tok_rows, span), 1)
    allowed = (key_pos >= begins) & (key_pos <= position)
    for k in range(1, reach + 1):
        pl.when(seq >= k)(kv_moves[k - 1].wait_recv)
    everything = kv[...].reshape(span, 2 * head_dim)
    keys, values = everything[:, :head_dim], everything[:, head_dim:]
    for h in range(query_width // head_dim):
        scores = lax.dot_general(
            queries[:, h * head_dim : (h + 1) * head_dim], keys,
            (((1,), (1,)), ((), ())), preferred_element_type=f32,
        ) * head_dim ** (-0.5)
        scores = jnp.where(allowed, scores, -1e30)
        weights = jnp.exp(scores - jnp.max(scores, axis=-1, keepdims=True))
        totals = jnp.sum(weights, axis=-1, keepdims=True)
        mixed = jnp.dot(weights.astype(bf16), values, preferred_element_type=f32)
        attended[:, h * head_dim : (h + 1) * head_dim] = (mixed / totals).astype(bf16)
    for distance in range(line):
        out_relay.b_lines(distance)
    out_relay.settle()

    n_dev = n_grp * n_seq
    out_width = attn_out.shape[1]
    out_loads = [
        pltpu.make_async_copy(out_all.at[i], out_v.at[i % AHEAD], out_sem.at[i % AHEAD])
        for i in range(n_dev)
    ]
    for i in range(AHEAD):
        out_loads[i].start()
    stores = []
    for c in range(n_seq):
        for j in range(n_grp):
            i = c * n_grp + j
            out_loads[i].wait()
            update = jnp.dot(attended[...], out_v[i % AHEAD], preferred_element_type=f32)
            if i + AHEAD < n_dev:
                out_loads[i + AHEAD].start()
            columns = slice(j * out_width, (j + 1) * out_width)
            held = chunk(c)
            held[:, columns] = (held[:, columns].astype(f32) + update).astype(bf16)
        stores.append(
            pltpu.make_async_copy(chunk(c), result.at[:, chunk_columns(c)], result_sem.at[c])
        )
        stores[-1].start()
    for store in stores:
        store.wait()
    first.end()
    second.end()
    for move in table_moves:
        move.wait_send()
    for k in range(1, reach + 1):
        pl.when(seq + k < n_seq)(kv_moves[k - 1].wait_send)
    relay.end()
    out_relay.end()


VMEM = pl.BlockSpec(memory_space=pltpu.VMEM)
SMEM = pl.BlockSpec(memory_space=pltpu.SMEM)
ANY = pl.BlockSpec(memory_space=pl.ANY)


def on_device(
    patches, piece_ids, vit_gain, vit_qkv, vit_out, merge_gain, merge_up, merge_down, dest,
    tokens, image_index, doc_lengths, attn_gain, attn_qkv, attn_out,
):
    rows, features = patches.shape
    n_seq, n_grp = lax.axis_size("seq"), lax.axis_size("grp")
    n_dev = n_seq * n_grp
    own = rows // 4
    capacity = own // (n_seq // 2)
    slots = n_seq * capacity
    reach = n_seq // 2
    line = n_seq // 2
    bf16, f32 = jnp.bfloat16, jnp.float32
    tok_rows = tokens.shape[0]
    query_width, out_width = attn_out.shape
    kv_width = attn_qkv.shape[1] - query_width
    down_width = merge_down.shape[1]
    dma = pltpu.SemaphoreType.DMA
    result, _ = pl.pallas_call(
        functools.partial(layer_kernel, n_grp, n_seq, capacity, reach),
        out_shape=(
            jax.ShapeDtypeStruct(tokens.shape, bf16),
            jax.ShapeDtypeStruct((n_dev,) + attn_out.shape, bf16),
        ),
        in_specs=[VMEM] * 6 + [SMEM] * 2 + [ANY] * 7,
        out_specs=(ANY, ANY),
        scratch_shapes=[
            pltpu.VMEM(vit_qkv.shape, bf16),
            pltpu.VMEM(vit_out.shape, bf16),
            pltpu.VMEM(merge_up.shape, bf16),
            pltpu.VMEM(merge_down.shape, bf16),
            pltpu.VMEM((n_dev,) + attn_qkv.shape, bf16),
            pltpu.VMEM((features // LANES, rows, LANES), f32),
            pltpu.VMEM((n_seq, own, 4 * features + LANES), bf16),
            pltpu.VMEM((n_seq, n_seq * own, merge_up.shape[1]), bf16),
            pltpu.VMEM((n_seq, slots, down_width), bf16),
            pltpu.VMEM((n_seq, slots, down_width), bf16),
            pltpu.VMEM((tok_rows, query_width), bf16),
            pltpu.VMEM((reach + 1, tok_rows, kv_width), bf16),
            pltpu.VMEM((tok_rows, query_width), bf16),
            pltpu.VMEM((AHEAD, query_width, out_width), bf16),
            dma((6,)), dma((n_seq,)), dma((n_seq,)), dma((AHEAD,)),
            dma((2, line)), dma((2, line)), dma((n_seq,)), dma((n_seq,)),
            dma((n_seq,)), dma((n_seq,)), dma((reach + 1,)), dma((reach + 1,)),
        ] + relay_scratch(n_dev) + relay_scratch(n_dev),
        compiler_params=pltpu.CompilerParams(
            collective_id=0, has_side_effects=True, vmem_limit_bytes=67000000
        ),
    )(
        patches, piece_ids, vit_gain, merge_gain, attn_gain, image_index, dest, doc_lengths,
        vit_qkv, vit_out, merge_up, merge_down, tokens, attn_qkv, attn_out,
    )
    return result


def solution(mesh):
    placed = (
        P(("grp", "seq"), None),
        P(("grp", "seq"), None),
        P(),
        P(),
        P(),
        P(),
        P(None, "seq"),
        P(None, "seq"),
        P(("grp", "seq")),
        P(("grp", "seq"), None),
        P(("grp", "seq")),
        P("grp", None),
        P(),
        P(("grp", "seq"), None),
        P(None, ("grp", "seq")),
    )
    return jax.shard_map(
        on_device, mesh=mesh, in_specs=placed, out_specs=P(("grp", "seq"), None), check_vma=False
    )
```

time: 214 us -> 150 us (0.70); the launches traced: 209 us -> 149 us
  Pallas kernels: 186 us -> 145 us
  matrix products: 12 us -> 0 us
  other arithmetic: 5.6 us -> 0 us
    pallas_call x3 -> x1, Pallas kernels: 186 us -> 145 us  [on_device(): pl.pallas_call(functools.partial(layer_kernel, n_grp, n_seq, capacity, re...]
    dot_general x2 -> x0, matrix products: 12 us -> none  [the longest x1 8.14 us: on_device(): jnp.dot(normed, qkv_all.reshape(-1, attn_qkv.shape[1]), preferred_element...]
    unnamed x8 -> x1, local copies, waits for them, and re-layouts: 0.02 us -> 4.64 us
    broadcast_in_dim x4 -> x0, local copies, waits for them, and re-layouts: 4.05 us -> none  [the longest x1 1.29 us: on_device(): merge_gain[None]]
    add x4 -> x0, other arithmetic: 2.5 us -> none  [the longest x2 1.85 us: on_device(): pieces = piece_ids.reshape(-1) + windows * WIN]
where the time goes in v1:
time: 150 us; the launch traced here: 149 us
  Pallas kernels  145 us (97%)
  local copies, waits for them, and re-layouts  4.64 us (3%)
    pallas_call x1, Pallas kernels, on_device(): pl.pallas_call(functools.partial(layer_kernel, n_grp, n_seq, capacity, re...  145 us
    unnamed x1, local copies, waits for them, and re-layouts  4.64 us

profile of v1, /device:TPU:25, one launch (start us, length us, event | category | flops | bytes accessed | tf_op | source)
XLA Modules:
  0.0 149.3 jit_solution(2171844270002401016)
XLA Ops:
  0.0 144.7 %shard_map.145 = (bf16[256,8192]{1,0:T(8,128)(2,1)}, bf16[32,512,256]{2,1,0:T(8,128)(2,1)}) custom-call(bf16[64,1280]{1,0:T(8,128)(2,1)} %patches.1, s32[1,64]{1,0:T(1,128)} %pieces.1, f32[1280]{0:T(1024)} %vit_gain.1, f32[1280]{0:T(1024)} %merge_gain.1, f32[8192]{0:T(1024)} %attn_gain.1, s32[256]{0:T(256)} %image_index.1, s32[16]{0:T(128)} %dest.1, ...), custom_call_target="tpu_custom_call" | custom-call | tf_op jit(solution)/shard_map/pallas_call | solution.py:587
  144.7 4.6 %copy.17 = bf16[256,8192]{1,0:T(8,128)(2,1)} copy(bf16[256,8192]{1,0:T(8,128)(2,1)} %get-tuple-element.6) | data formatting | bytes 8388608

commit v2 on v1

--- a/solution.py
+++ b/solution.py
@@ -12,7 +12,8 @@
 WIN = 64
 LANES = 128
 EPSILON = 1e-06
-AHEAD = 4
+AHEAD = 8
+PLAN = {0: ('wsx', 'ra0', 'ro1'), (1, 2): ('ro2',), 6: ('ra1', 'ro3', 'wsy', 'wsz', 'wsc'), (2, 2): ('ra2',), 10: ('ra3', 'wo1', 'wa0'), 11: ('rb0', 'rb1', 'rb2', 'rb3', 'wo2'), 12: ('wa1', 'wo3'), 13: ('wa2',), 14: ('wa3', 'wb0'), 16: ('wb1',), 17: ('wb2', 'wb3')}
 MESH = pl.DeviceIdType.MESH
 
 
@@ -42,11 +43,12 @@
 
 
 class Relay:
-    def __init__(self, n_seq, shard, full, first, local_sem, recv_sem, send_sem):
+    def __init__(self, n_seq, shard, full, first, plane, local_sem, recv_sem, send_sem):
         self.n_seq, self.shard, self.full = n_seq, shard, full
         self.local_sem, self.recv_sem, self.send_sem = local_sem, recv_sem, send_sem
         self.line = n_seq // 2
         self.grp, self.seq = lax.axis_index("grp"), lax.axis_index("seq")
+        self.plane, self.first, self.done = plane, first, []
         self.place, self.side = self.seq // 2, lax.rem(self.seq, 2)
         far = flip(self.grp, 2)
         self.far = far
@@ -78,21 +80,25 @@
     def me(self):
         return (self.grp, self.seq)
 
-    def begin(self):
+    def launch(self, kind):
         slot = self.slot(self.me(), self.place)
-        pltpu.make_async_copy(self.shard, self.full.at[slot], self.local_sem).start()
-
-        @pl.when(self.place + 1 < self.line)
-        def _():
-            self.copy(slot, 0, self.up(), True).start()
-
-        @pl.when(self.place > 0)
-        def _():
-            self.copy(slot, 1, self.down(), True).start()
-
-        self.copy(slot, 2, self.a_dev, True).start()
-        self.copy(slot, 3, self.b_dev, True).start()
-        self.copy(slot, 4, self.core_dev, True).start()
+        if kind == "c":
+            pltpu.make_async_copy(self.shard, self.full.at[slot], self.local_sem).start()
+            self.copy(slot, 4, self.core_dev, True).start()
+        elif kind == "z":
+
+            @pl.when(self.place + 1 < self.line)
+            def _():
+                self.copy(slot, 0, self.up(), True).start()
+
+            @pl.when(self.place > 0)
+            def _():
+                self.copy(slot, 1, self.down(), True).start()
+
+        else:
+            a_way = self.first if kind == "x" else jnp.logical_not(self.first)
+            device = (self.far, self.seq) if kind == "x" else (self.grp, flip(self.seq, 1))
+            self.copy(slot, jnp.where(a_way, 2, 3), device, True).start()
 
     def spots(self, distance):
         low, high = self.place - distance, self.place + distance
@@ -100,30 +106,36 @@
             return [(self.place, None, None)]
         return [(low, low >= 0, True), (high, high < self.line, False)]
 
-    def visit(self, base, distance, ways, finish=False):
+    def pass_on(self, slot, way, device, guard, finish):
+        def act():
+            move = self.copy(slot, way, device)
+            move.wait_send() if finish else move.start()
+
+        if guard is True:
+            act()
+        elif guard is not False:
+            pl.when(guard)(act)
+
+    def along(self, guard, room):
+        if guard is True:
+            return room
+        return False if guard is False else guard & room
+
+    def visit(self, base, distance, ways, line, finish=False):
         for place, there, upward in self.spots(distance):
 
             def act(place=place, upward=upward):
                 slot = self.slot(base, place)
-                own_core = base is not None
                 if not finish:
                     self.copy(slot, 4, self.core_dev).wait_recv()
-                for way, device in ways:
-                    move = self.copy(slot, way, device)
-                    move.wait_send() if finish else move.start()
-                if upward is True and "z" in self.mode:
-
-                    @pl.when(self.place + 1 < self.line)
-                    def _():
-                        move = self.copy(slot, 0, self.up())
-                        move.wait_send() if finish else move.start()
-
-                if upward is False and "z" in self.mode:
-
-                    @pl.when(self.place > 0)
-                    def _():
-                        move = self.copy(slot, 1, self.down())
-                        move.wait_send() if finish else move.start()
+                if upward is not False:
+                    room = self.along(line, self.place + 1 < self.line)
+                    self.pass_on(slot, 0, self.up(), room, finish)
+                if upward is not True:
+                    room = self.along(line, self.place > 0)
+                    self.pass_on(slot, 1, self.down(), room, finish)
+                for way, device, guard in ways:
+                    self.pass_on(slot, way, device, guard, finish)
 
             if there is None:
                 act()
@@ -131,20 +143,36 @@
                 pl.when(there)(act)
 
     def own_line(self, distance, finish=False):
-        self.mode = "z"
-        self.visit(
-            self.me(), distance,
-            [(2, self.a_dev), (3, self.b_dev), (4, self.core_dev)], finish,
-        )
+        spread = self.plane
+        beyond = (not spread) if isinstance(spread, bool) else jnp.logical_not(spread)
+        ways = [(3, self.b_dev, True), (2, self.a_dev, beyond), (4, self.core_dev, True)]
+        self.visit(self.me(), distance, ways, True, finish)
 
     def a_line(self, distance, finish=False):
-        self.mode = ""
-        self.visit(self.a_dev, distance, [(3, self.b_dev), (4, self.core_dev)], finish)
+        ways = [(3, self.b_dev, True), (4, self.core_dev, True)]
+        self.visit(self.a_dev, distance, ways, self.plane, finish)
 
     def b_lines(self, distance, finish=False):
-        self.mode = ""
-        self.visit(self.b_dev, distance, [(4, self.core_dev)], finish)
-        self.visit(self.ab_dev, distance, [(4, self.core_dev)], finish)
+        ways = [(4, self.core_dev, True)]
+        self.visit(self.b_dev, distance, ways, False, finish)
+        self.visit(self.ab_dev, distance, ways, False, finish)
+
+    def run(self, name):
+        if name in self.done:
+            return
+        self.done.append(name)
+        if name[0] == "s":
+            self.launch(name[1])
+        elif int(name[1:]) < self.line:
+            actions = {"o": self.own_line, "a": self.a_line, "b": self.b_lines}
+            actions[name[0]](int(name[1:]))
+
+    def flush(self):
+        for kind in "xyzc":
+            self.run("s" + kind)
+        for kind in "oab":
+            for distance in range(kind == "o", self.line):
+                self.run(kind + str(distance))
 
     def end(self):
         slot = self.slot(self.me(), self.place)
@@ -341,8 +369,16 @@
     for load in vit_loads + [vit_out_load]:
         load.start()
     greet(n_seq, (flip(grp, 1), flip(grp, 2)))
-    relay = Relay(n_seq, attn_qkv, qkv_all, False, *relay_sems[:3])
-    relay.begin()
+    core = lax.rem(grp, 2)
+    relay = Relay(n_seq, attn_qkv, qkv_all, False, False, *relay_sems[:3])
+    for kind in "xyzc":
+        relay.run("s" + kind)
+    out_relay = Relay(n_seq, attn_out, out_all, core == 0, core == 1, *relay_sems[3:])
+
+    def at(point):
+        for name in PLAN.get(point, ()):
+            (out_relay if name[0] == "w" else relay).run(name[1:])
+
 
     chunk_width = merge_down.shape[1]
     per_row = vit_qkv.shape[1] // chunk_width
@@ -373,6 +409,7 @@
         for c in range(n_seq)
     ]
     mixture = window_attention(projected, pieces[...], features)
+    at(0)
     vit_out_load.wait()
     residual = residual + jnp.dot(mixture, vit_out_v[...], preferred_element_type=f32)
     merged_in = rms_scale(residual, merge_gain[...].reshape(1, features))
@@ -389,17 +426,16 @@
     gathered[seq, :, 4 * features :] = row_codes(dest, own, capacity).astype(bf16)
     first = Gather(n_seq, gathered, gather_send, gather_recv)
     first.begin()
-    relay.own_line(1)
+    at(1)
     for load in token_loads:
         load.start()
     line = n_seq // 2
     for distance in range(1, line):
         first.forward(distance)
-    for distance in range(2, line):
-        relay.own_line(distance)
-    relay.a_line(0)
+        at((1, distance))
+    first.settle()
+    at(5)
     up_load.wait()
-    first.settle()
 
     all_rows = n_seq * own
     entry = gathered[:, :, : 4 * features].reshape(all_rows, 4 * features)
@@ -407,6 +443,7 @@
     hidden[seq] = (0.5 * pre * (1.0 + lax.erf(pre * 0.5**0.5))).astype(bf16)
     second = Gather(n_seq, hidden, hidden_send, hidden_recv)
     second.begin()
+    at(6)
 
     codes = gathered[:, :, 4 * features :].reshape(all_rows, LANES).astype(f32)[:, :1]
     row = lax.broadcasted_iota(jnp.int32, (all_rows, 1), 0).astype(f32)
@@ -420,7 +457,7 @@
 
     for distance in range(1, line):
         second.forward(distance)
-        relay.a_line(distance)
+        at((2, distance))
     down_load.wait()
     part_width = hidden.shape[2]
 
@@ -434,6 +471,7 @@
     total = term(side)
     for p in range(1, line):
         total = total + term(2 * p + side)
+    at(10)
     second.settle()
     for p in range(line):
         total = total + term(2 * p + 1 - side)
@@ -443,11 +481,7 @@
     table_moves = swap(
         n_seq, lambda to: stage.at[to], lambda me: landed.at[me], table_send, table_recv
     )
-    out_relay = Relay(n_seq, attn_out, out_all, lax.rem(grp, 2) == 0, *relay_sems[3:])
-    out_relay.begin()
-    for distance in range(line):
-        relay.b_lines(distance)
-
+    at(11)
     slot = lax.broadcasted_iota(jnp.int32, (slots, tok_rows), 0)
     picked = jnp.where(slot == image_index[...].reshape(1, tok_rows), 1.0, 0.0)
     picker = jnp.transpose(picked)
@@ -455,6 +489,7 @@
     picker = picker.astype(bf16)
     for move in table_moves:
         move.wait_recv()
+    at(12)
     square = jnp.zeros((tok_rows, 1), f32)
     for c in range(n_seq):
         token_loads[c].wait()
@@ -462,8 +497,9 @@
         layer_in = jnp.where(pictured, image, chunk(c)[...].astype(f32))
         chunk(c)[...] = layer_in.astype(bf16)
         square = square + jnp.sum(layer_in * layer_in, axis=1, keepdims=True)
-    out_relay.own_line(1)
     scale = lax.rsqrt(square / (n_seq * chunk_width) + EPSILON)
+    at(13)
+    relay.flush()
     relay.settle()
     shard_rows, qkv_width = attn_qkv.shape
     attn_projected = jnp.zeros((tok_rows, qkv_width), f32)
@@ -475,31 +511,47 @@
     query_width = attn_out.shape[0]
     queries[...] = attn_projected[:, :query_width].astype(bf16)
     kv[reach] = attn_projected[:, query_width:].astype(bf16)
-    kv_moves = []
+    half = reach // 2
+    post = seq // 2
+
+    def kv_copy(k_from, k_to, way, device):
+        return pltpu.make_async_remote_copy(
+            src_ref=kv.at[reach - k_from],
+            dst_ref=kv.at[reach - k_to],
+            send_sem=kv_send.at[way],
+            recv_sem=kv_recv.at[k_to],
+            device_id=device,
+            device_id_type=MESH,
+        )
+
+    mate = (grp, flip(seq, 1))
+    kv_moves = [(side == 0, kv_copy(0, 1, 0, mate))]
+    for d in range(1, half + 1):
+        ahead = (grp, jnp.minimum(seq + 2 * d, n_seq - 1))
+        kv_moves.append((post + d < line, kv_copy(0, 2 * d, d, ahead)))
+    for there, move in kv_moves:
+        pl.when(there)(move.start)
     for k in range(1, reach + 1):
-        kv_moves.append(
-            pltpu.make_async_remote_copy(
-                src_ref=kv.at[reach],
-                dst_ref=kv.at[reach - k],
-                send_sem=kv_send.at[k],
-                recv_sem=kv_recv.at[k],
-                device_id=(grp, lax.rem(seq + k, n_seq)),
-                device_id_type=MESH,
-            )
-        )
-        pl.when(seq + k < n_seq)(kv_moves[-1].start)
 
         @pl.when(seq < k)
         def _():
             kv[reach - k] = jnp.zeros(kv.shape[1:], bf16)
 
-    for distance in range(2, line):
-        out_relay.own_line(distance)
-    for distance in range(line):
-        out_relay.a_line(distance)
-
+    def kv_arrival(k):
+        pl.when(seq >= k)(kv_copy(0, k, 0, mate).wait_recv)
+
+    at(14)
+    for d in range(1, half + 1):
+        kv_arrival(2 * d)
+        there = (post >= d) & ((side == 1) | (d < half))
+        move = kv_copy(2 * d, jnp.minimum(2 * d + 1 - 2 * side, reach), half + d, mate)
+        kv_moves.append((there, move))
+        pl.when(there)(move.start)
+
+    at(15)
     head_dim = kv.shape[2] // 2
     span = (reach + 1) * tok_rows
+    at(16)
     position = seq * tok_rows + lax.broadcasted_iota(jnp.int32, (tok_rows, 1), 0)
     begins = jnp.zeros((tok_rows, 1), jnp.int32)
     total_length = jnp.int32(0)
@@ -508,8 +560,8 @@
         total_length = total_length + doc_lengths[0, k]
     key_pos = (seq - reach) * tok_rows + lax.broadcasted_iota(jnp.int32, (tok_rows, span), 1)
     allowed = (key_pos >= begins) & (key_pos <= position)
-    for k in range(1, reach + 1):
-        pl.when(seq >= k)(kv_moves[k - 1].wait_recv)
+    for k in range(1, reach, 2):
+        kv_arrival(k)
     everything = kv[...].reshape(span, 2 * head_dim)
     keys, values = everything[:, :head_dim], everything[:, head_dim:]
     for h in range(query_width // head_dim):
@@ -522,25 +574,29 @@
         totals = jnp.sum(weights, axis=-1, keepdims=True)
         mixed = jnp.dot(weights.astype(bf16), values, preferred_element_type=f32)
         attended[:, h * head_dim : (h + 1) * head_dim] = (mixed / totals).astype(bf16)
-    for distance in range(line):
-        out_relay.b_lines(distance)
+    at(17)
+    out_relay.flush()
     out_relay.settle()
 
     n_dev = n_grp * n_seq
     out_width = attn_out.shape[1]
+    streamed = out_width % LANES != 0
+    ahead = AHEAD if streamed else 0
     out_loads = [
         pltpu.make_async_copy(out_all.at[i], out_v.at[i % AHEAD], out_sem.at[i % AHEAD])
-        for i in range(n_dev)
+        for i in range(n_dev if streamed else 0)
     ]
-    for i in range(AHEAD):
+    for i in range(ahead):
         out_loads[i].start()
     stores = []
     for c in range(n_seq):
         for j in range(n_grp):
             i = c * n_grp + j
-            out_loads[i].wait()
-            update = jnp.dot(attended[...], out_v[i % AHEAD], preferred_element_type=f32)
-            if i + AHEAD < n_dev:
+            if streamed:
+                out_loads[i].wait()
+            weight = out_v[i % AHEAD] if streamed else out_all[i]
+            update = jnp.dot(attended[...], weight, preferred_element_type=f32)
+            if streamed and i + AHEAD < n_dev:
                 out_loads[i + AHEAD].start()
             columns = slice(j * out_width, (j + 1) * out_width)
             held = chunk(c)
@@ -555,8 +611,8 @@
     second.end()
     for move in table_moves:
         move.wait_send()
-    for k in range(1, reach + 1):
-        pl.when(seq + k < n_seq)(kv_moves[k - 1].wait_send)
+    for there, move in kv_moves:
+        pl.when(there)(move.wait_send)
     relay.end()
     out_relay.end()
 
@@ -584,15 +640,19 @@
     kv_width = attn_qkv.shape[1] - query_width
     down_width = merge_down.shape[1]
     dma = pltpu.SemaphoreType.DMA
-    result, _ = pl.pallas_call(
+    streamed = out_width % LANES != 0
+    out_all_shape = (n_dev,) + attn_out.shape
+    outputs = [jax.ShapeDtypeStruct(tokens.shape, bf16)]
+    held = [pltpu.VMEM(out_all_shape, bf16)]
+    if streamed:
+        outputs.append(jax.ShapeDtypeStruct(out_all_shape, bf16))
+        held = []
+    results = pl.pallas_call(
         functools.partial(layer_kernel, n_grp, n_seq, capacity, reach),
-        out_shape=(
-            jax.ShapeDtypeStruct(tokens.shape, bf16),
-            jax.ShapeDtypeStruct((n_dev,) + attn_out.shape, bf16),
-        ),
+        out_shape=tuple(outputs),
         in_specs=[VMEM] * 6 + [SMEM] * 2 + [ANY] * 7,
-        out_specs=(ANY, ANY),
-        scratch_shapes=[
+        out_specs=(ANY,) * len(outputs),
+        scratch_shapes=held + [
             pltpu.VMEM(vit_qkv.shape, bf16),
             pltpu.VMEM(vit_out.shape, bf16),
             pltpu.VMEM(merge_up.shape, bf16),
@@ -606,19 +666,19 @@
             pltpu.VMEM((tok_rows, query_width), bf16),
             pltpu.VMEM((reach + 1, tok_rows, kv_width), bf16),
             pltpu.VMEM((tok_rows, query_width), bf16),
-            pltpu.VMEM((AHEAD, query_width, out_width), bf16),
+            pltpu.VMEM((AHEAD, query_width if streamed else 16, out_width), bf16),
             dma((6,)), dma((n_seq,)), dma((n_seq,)), dma((AHEAD,)),
             dma((2, line)), dma((2, line)), dma((n_seq,)), dma((n_seq,)),
-            dma((n_seq,)), dma((n_seq,)), dma((reach + 1,)), dma((reach + 1,)),
+            dma((n_seq,)), dma((n_seq,)), dma((reach + 2,)), dma((reach + 1,)),
         ] + relay_scratch(n_dev) + relay_scratch(n_dev),
         compiler_params=pltpu.CompilerParams(
-            collective_id=0, has_side_effects=True, vmem_limit_bytes=67000000
+            collective_id=0, has_side_effects=True, vmem_limit_bytes=67043328
         ),
     )(
         patches, piece_ids, vit_gain, merge_gain, attn_gain, image_index, dest, doc_lengths,
         vit_qkv, vit_out, merge_up, merge_down, tokens, attn_qkv, attn_out,
     )
-    return result
+    return results[0]
 
 
 def solution(mesh):

time: 150 us -> 136 us (0.907)
  Pallas kernels: 145 us -> 131 us
    pallas_call x1, Pallas kernels: 145 us -> 131 us  [on_device(): pl.pallas_call(functools.partial(layer_kernel, n_grp, n_seq, capacity, re...]
where the time goes in v2:
time: 136 us
  Pallas kernels  131 us (96%)
  local copies, waits for them, and re-layouts  4.64 us (3%)
    pallas_call x1, Pallas kernels, on_device(): pl.pallas_call(functools.partial(layer_kernel, n_grp, n_seq, capacity, re...  131 us
    unnamed x1, local copies, waits for them, and re-layouts  4.64 us

profile of v2, /device:TPU:25, one launch (start us, length us, event | category | flops | bytes accessed | tf_op | source)
XLA Modules:
  0.0 135.9 jit_solution(6262626630014687715)
XLA Ops:
  0.0 131.3 %shard_map.145 = bf16[256,8192]{1,0:T(8,128)(2,1)} custom-call(bf16[64,1280]{1,0:T(8,128)(2,1)} %patches.1, s32[1,64]{1,0:T(1,128)} %pieces.1, f32[1280]{0:T(1024)} %vit_gain.1, f32[1280]{0:T(1024)} %merge_gain.1, f32[8192]{0:T(1024)} %attn_gain.1, s32[256]{0:T(256)} %image_index.1, s32[16]{0:T(128)} %dest.1, s32[1,4]{1,0:T(1,128)} %doc_lengths.1, ...), custom_call_target="tpu_custom_call" | custom-call | tf_op jit(solution)/shard_map/pallas_call | solution.py:650
  131.3 4.6 %copy.17 = bf16[256,8192]{1,0:T(8,128)(2,1)} copy(bf16[256,8192]{1,0:T(8,128)(2,1)} %shard_map.145) | data formatting | bytes 8388608

commit v3 on v2

--- a/solution.py
+++ b/solution.py
@@ -13,7 +13,7 @@
 LANES = 128
 EPSILON = 1e-06
 AHEAD = 8
-PLAN = {0: ('wsx', 'ra0', 'ro1'), (1, 2): ('ro2',), 6: ('ra1', 'ro3', 'wsy', 'wsz', 'wsc'), (2, 2): ('ra2',), 10: ('ra3', 'wo1', 'wa0'), 11: ('rb0', 'rb1', 'rb2', 'rb3', 'wo2'), 12: ('wa1', 'wo3'), 13: ('wa2',), 14: ('wa3', 'wb0'), 16: ('wb1',), 17: ('wb2', 'wb3')}
+PLAN = {0: ('wsx', 'ra0', 'ro1xc'), 1: ('ro1z', 'ro1y'), (1, 2): ('ro2',), 6: ('ra1', 'ro3', 'wsy', 'wsz', 'wsc'), (2, 2): ('ra2',), 10: ('ra3', 'wo1', 'wa0'), 11: ('rb0', 'rb1', 'rb2', 'rb3', 'wo2'), 12: ('wa1', 'wo3'), 14: ('wa2',), 15: ('wa3',), 16: ('wb0', 'wb1'), 17: ('wb2', 'wb3')}
 MESH = pl.DeviceIdType.MESH
 
 
@@ -40,6 +40,26 @@
 
 def flip(index, bit):
     return index + bit - 2 * bit * lax.rem(index // bit, 2)
+
+
+def opposite(flag):
+    return (not flag) if isinstance(flag, bool) else jnp.logical_not(flag)
+
+
+def either(left, right):
+    if left is True or right is True:
+        return True
+    if left is False:
+        return right
+    return left if right is False else left | right
+
+
+def both(left, right):
+    if left is False or right is False:
+        return False
+    if left is True:
+        return right
+    return left if right is True else left & right
 
 
 class Relay:
@@ -96,9 +116,8 @@
                 self.copy(slot, 1, self.down(), True).start()
 
         else:
-            a_way = self.first if kind == "x" else jnp.logical_not(self.first)
-            device = (self.far, self.seq) if kind == "x" else (self.grp, flip(self.seq, 1))
-            self.copy(slot, jnp.where(a_way, 2, 3), device, True).start()
+            way, device = self.side_way(kind)
+            self.copy(slot, way, device, True).start()
 
     def spots(self, distance):
         low, high = self.place - distance, self.place + distance
@@ -116,63 +135,75 @@
         elif guard is not False:
             pl.when(guard)(act)
 
-    def along(self, guard, room):
-        if guard is True:
-            return room
-        return False if guard is False else guard & room
-
-    def visit(self, base, distance, ways, line, finish=False):
+    def visit(self, base, distance, ways, finish):
         for place, there, upward in self.spots(distance):
 
             def act(place=place, upward=upward):
                 slot = self.slot(base, place)
-                if not finish:
-                    self.copy(slot, 4, self.core_dev).wait_recv()
-                if upward is not False:
-                    room = self.along(line, self.place + 1 < self.line)
-                    self.pass_on(slot, 0, self.up(), room, finish)
-                if upward is not True:
-                    room = self.along(line, self.place > 0)
-                    self.pass_on(slot, 1, self.down(), room, finish)
-                for way, device, guard in ways:
-                    self.pass_on(slot, way, device, guard, finish)
+                for kind, guard in ways:
+                    if kind == "r":
+                        self.copy(slot, 4, self.core_dev).wait_recv()
+                    elif kind == "z":
+                        if upward is not False:
+                            room = both(guard, self.place + 1 < self.line)
+                            self.pass_on(slot, 0, self.up(), room, finish)
+                        if upward is not True:
+                            room = both(guard, self.place > 0)
+                            self.pass_on(slot, 1, self.down(), room, finish)
+                    elif kind == "c":
+                        self.pass_on(slot, 4, self.core_dev, guard, finish)
+                    else:
+                        self.pass_on(slot, *self.side_way(kind), guard, finish)
 
             if there is None:
                 act()
             else:
                 pl.when(there)(act)
 
-    def own_line(self, distance, finish=False):
-        spread = self.plane
-        beyond = (not spread) if isinstance(spread, bool) else jnp.logical_not(spread)
-        ways = [(3, self.b_dev, True), (2, self.a_dev, beyond), (4, self.core_dev, True)]
-        self.visit(self.me(), distance, ways, True, finish)
-
-    def a_line(self, distance, finish=False):
-        ways = [(3, self.b_dev, True), (4, self.core_dev, True)]
-        self.visit(self.a_dev, distance, ways, self.plane, finish)
-
-    def b_lines(self, distance, finish=False):
-        ways = [(4, self.core_dev, True)]
-        self.visit(self.b_dev, distance, ways, False, finish)
-        self.visit(self.ab_dev, distance, ways, False, finish)
+    def side_way(self, kind):
+        a_way = self.first if kind == "x" else opposite(self.first)
+        device = (self.far, self.seq) if kind == "x" else (self.grp, flip(self.seq, 1))
+        return jnp.where(a_way, 2, 3), device
+
+    def forward(self, kind, distance, ways, finish=False):
+        later = opposite(self.plane)
+        guards = {
+            "o": {
+                "x": either(opposite(self.first), later), "y": either(self.first, later),
+                "z": True, "c": True,
+            },
+            "a": {"x": opposite(self.first), "y": self.first, "z": self.plane, "c": True},
+            "b": {"c": True},
+        }[kind]
+        chosen = [("r", True)] if "r" in ways else []
+        chosen += [(way, guards[way]) for way in ways if way in guards]
+        bases = {"o": [self.me()], "a": [self.a_dev], "b": [self.b_dev, self.ab_dev]}[kind]
+        for base in bases:
+            self.visit(base, distance, chosen, finish)
 
     def run(self, name):
-        if name in self.done:
+        if name[0] == "s":
+            if name not in self.done:
+                self.launch(name[1])
+            self.done.append(name)
             return
-        self.done.append(name)
-        if name[0] == "s":
-            self.launch(name[1])
-        elif int(name[1:]) < self.line:
-            actions = {"o": self.own_line, "a": self.a_line, "b": self.b_lines}
-            actions[name[0]](int(name[1:]))
+        kind, distance = name[0], int(name[1])
+        self.run_ways(kind, distance, name[2:] or "xyzc")
+
+    def run_ways(self, kind, distance, ways):
+        if distance >= self.line:
+            return
+        ways = [way for way in "r" + ways if (kind, distance, way) not in self.done]
+        self.done += [(kind, distance, way) for way in ways]
+        if ways:
+            self.forward(kind, distance, ways)
 
     def flush(self):
         for kind in "xyzc":
             self.run("s" + kind)
         for kind in "oab":
             for distance in range(kind == "o", self.line):
-                self.run(kind + str(distance))
+                self.run_ways(kind, distance, "xyzc")
 
     def end(self):
         slot = self.slot(self.me(), self.place)
@@ -188,11 +219,9 @@
         self.copy(slot, 2, self.a_dev, True).wait_send()
         self.copy(slot, 3, self.b_dev, True).wait_send()
         self.copy(slot, 4, self.core_dev, True).wait_send()
-        for distance in range(self.line):
-            if distance:
-                self.own_line(distance, True)
-            self.a_line(distance, True)
-            self.b_lines(distance, True)
+        for kind in "oab":
+            for distance in range(kind == "o", self.line):
+                self.forward(kind, distance, "xyzc", True)
 
     def settle(self):
         slot = self.slot(self.me(), self.place)

time: 136 us -> 130 us (0.956)
  Pallas kernels: 131 us -> 125 us
    pallas_call x1, Pallas kernels: 131 us -> 125 us  [on_device(): pl.pallas_call(functools.partial(layer_kernel, n_grp, n_seq, capacity, re...]
where the time goes in v3:
time: 130 us
  Pallas kernels  125 us (96%)
  local copies, waits for them, and re-layouts  4.64 us (4%)
    pallas_call x1, Pallas kernels, on_device(): pl.pallas_call(functools.partial(layer_kernel, n_grp, n_seq, capacity, re...  125 us
    unnamed x1, local copies, waits for them, and re-layouts  4.64 us

profile of v3, /device:TPU:25, one launch (start us, length us, event | category | flops | bytes accessed | tf_op | source)
XLA Modules:
  0.0 129.8 jit_solution(3741197561554361562)
XLA Ops:
  0.0 125.2 %shard_map.145 = bf16[256,8192]{1,0:T(8,128)(2,1)} custom-call(bf16[64,1280]{1,0:T(8,128)(2,1)} %patches.1, s32[1,64]{1,0:T(1,128)} %pieces.1, f32[1280]{0:T(1024)} %vit_gain.1, f32[1280]{0:T(1024)} %merge_gain.1, f32[8192]{0:T(1024)} %attn_gain.1, s32[256]{0:T(256)} %image_index.1, s32[16]{0:T(128)} %dest.1, s32[1,4]{1,0:T(1,128)} %doc_lengths.1, ...), custom_call_target="tpu_custom_call" | custom-call | tf_op jit(solution)/shard_map/pallas_call | solution.py:679
  125.2 4.6 %copy.17 = bf16[256,8192]{1,0:T(8,128)(2,1)} copy(bf16[256,8192]{1,0:T(8,128)(2,1)} %shard_map.145) | data formatting | bytes 8388608

commit v4 on v3

--- a/solution.py
+++ b/solution.py
@@ -13,7 +13,7 @@
 LANES = 128
 EPSILON = 1e-06
 AHEAD = 8
-PLAN = {0: ('wsx', 'ra0', 'ro1xc'), 1: ('ro1z', 'ro1y'), (1, 2): ('ro2',), 6: ('ra1', 'ro3', 'wsy', 'wsz', 'wsc'), (2, 2): ('ra2',), 10: ('ra3', 'wo1', 'wa0'), 11: ('rb0', 'rb1', 'rb2', 'rb3', 'wo2'), 12: ('wa1', 'wo3'), 14: ('wa2',), 15: ('wa3',), 16: ('wb0', 'wb1'), 17: ('wb2', 'wb3')}
+PLAN = {0: ('wsx', 'ra0xc'), 1: ('ro1y', 'ro1xc'), (1, 2): (), 6: ('ra1', 'ro3', 'wsy', 'wsz', 'wsc'), (2, 2): ('ra2',), 10: ('ra3', 'wo1', 'wa0'), 11: ('rb0', 'rb1', 'rb2', 'rb3', 'wo2'), (1, 1): ('ro1z',), (1, 3): ('ro2',), 12: ('wa1', 'wo3'), 14: ('wa2',), 15: ('wa3',), 16: ('wb0', 'wb1'), 17: ('wb2', 'wb3')}
 MESH = pl.DeviceIdType.MESH
 
 
@@ -257,26 +257,35 @@
         return (self.grp, flip(self.seq, 1))
 
     def begin(self, finish=False):
-        for place in range(self.line):
-
-            @pl.when(self.place != place)
+        for step in (1, -1):
+            to = self.place + step
+
+            @pl.when((to >= 0) & (to < self.line))
             def _():
-                move = self.copy(self.seq, 0, place, (self.grp, 2 * place + self.side))
+                move = self.copy(self.seq, 1 + step, self.place, (self.grp, self.seq + 2 * step))
                 move.wait_send() if finish else move.start()
 
         move = self.copy(self.seq, 1, self.place, self.across())
         move.wait_send() if finish else move.start()
 
-    def forward(self, distance):
+    def forward(self, distance, finish=False):
         low, high = self.place - distance, self.place + distance
-        for place, there in ((low, low >= 0), (high, high < self.line)):
+        for place, there, step in ((low, low >= 0, 1), (high, high < self.line, -1)):
 
             @pl.when(there)
             def _():
                 slot = 2 * place + self.side
+                to = self.place + step
                 move = self.copy(slot, 1, place, self.across())
-                move.wait_recv()
-                move.start()
+                if not finish:
+                    move.wait_recv()
+
+                @pl.when((to >= 0) & (to < self.line))
+                def _():
+                    onward = self.copy(slot, 1 + step, place, (self.grp, self.seq + 2 * step))
+                    onward.wait_send() if finish else onward.start()
+
+                move.wait_send() if finish else move.start()
 
     def settle(self):
         for place in range(self.line):
@@ -285,12 +294,8 @@
 
     def end(self):
         self.begin(True)
-        for place in range(self.line):
-
-            @pl.when(self.place != place)
-            def _():
-                slot = 2 * place + self.side
-                self.copy(slot, 1, place, self.across()).wait_send()
+        for distance in range(1, self.line):
+            self.forward(distance, True)
 
 
 def relay_scratch(n_dev):
@@ -516,16 +521,21 @@
     picker = jnp.transpose(picked)
     pictured = jnp.sum(picker, axis=1, keepdims=True) > 0.5
     picker = picker.astype(bf16)
-    for move in table_moves:
-        move.wait_recv()
+    square = jnp.zeros((tok_rows, 1), f32)
+    for load in token_loads:
+        load.wait()
+    for k in range(n_seq):
+        if k:
+            table_moves[k - 1].wait_recv()
+        c = lax.rem(seq - k + n_seq, n_seq)
+        rows_at = pl.multiple_of((c // per_row) * tok_rows, tok_rows)
+        columns_at = pl.multiple_of((c % per_row) * chunk_width, chunk_width)
+        held = wide_v.at[pl.ds(rows_at, tok_rows), pl.ds(columns_at, chunk_width)]
+        image = jnp.dot(picker, landed[c], preferred_element_type=f32)
+        layer_in = jnp.where(pictured, image, held[...].astype(f32))
+        held[...] = layer_in.astype(bf16)
+        square = square + jnp.sum(layer_in * layer_in, axis=1, keepdims=True)
     at(12)
-    square = jnp.zeros((tok_rows, 1), f32)
-    for c in range(n_seq):
-        token_loads[c].wait()
-        image = jnp.dot(picker, landed[c], preferred_element_type=f32)
-        layer_in = jnp.where(pictured, image, chunk(c)[...].astype(f32))
-        chunk(c)[...] = layer_in.astype(bf16)
-        square = square + jnp.sum(layer_in * layer_in, axis=1, keepdims=True)
     scale = lax.rsqrt(square / (n_seq * chunk_width) + EPSILON)
     at(13)
     relay.flush()
@@ -697,7 +707,7 @@
             pltpu.VMEM((tok_rows, query_width), bf16),
             pltpu.VMEM((AHEAD, query_width if streamed else 16, out_width), bf16),
             dma((6,)), dma((n_seq,)), dma((n_seq,)), dma((AHEAD,)),
-            dma((2, line)), dma((2, line)), dma((n_seq,)), dma((n_seq,)),
+            dma((3, line)), dma((3, line)), dma((n_seq,)), dma((n_seq,)),
             dma((n_seq,)), dma((n_seq,)), dma((reach + 2,)), dma((reach + 1,)),
         ] + relay_scratch(n_dev) + relay_scratch(n_dev),
         compiler_params=pltpu.CompilerParams(

time: 130 us -> 126 us (0.969)
  Pallas kernels: 125 us -> 121 us
    pallas_call x1, Pallas kernels: 125 us -> 121 us  [on_device(): pl.pallas_call(functools.partial(layer_kernel, n_grp, n_seq, capacity, re...]
where the time goes in v4:
time: 126 us
  Pallas kernels  121 us (96%)
  local copies, waits for them, and re-layouts  4.64 us (4%)
    pallas_call x1, Pallas kernels, on_device(): pl.pallas_call(functools.partial(layer_kernel, n_grp, n_seq, capacity, re...  121 us
    unnamed x1, local copies, waits for them, and re-layouts  4.64 us

profile of v4, /device:TPU:25, one launch (start us, length us, event | category | flops | bytes accessed | tf_op | source)
XLA Modules:
  0.0 125.8 jit_solution(2132707135606614721)
XLA Ops:
  0.0 121.1 %shard_map.145 = bf16[256,8192]{1,0:T(8,128)(2,1)} custom-call(bf16[64,1280]{1,0:T(8,128)(2,1)} %patches.1, s32[1,64]{1,0:T(1,128)} %pieces.1, f32[1280]{0:T(1024)} %vit_gain.1, f32[1280]{0:T(1024)} %merge_gain.1, f32[8192]{0:T(1024)} %attn_gain.1, s32[256]{0:T(256)} %image_index.1, s32[16]{0:T(128)} %dest.1, s32[1,4]{1,0:T(1,128)} %doc_lengths.1, ...), custom_call_target="tpu_custom_call" | custom-call | tf_op jit(solution)/shard_map/pallas_call | solution.py:689
  121.1 4.6 %copy.17 = bf16[256,8192]{1,0:T(8,128)(2,1)} copy(bf16[256,8192]{1,0:T(8,128)(2,1)} %shard_map.145) | data formatting | bytes 8388608

commit v5 on v4

--- a/solution.py
+++ b/solution.py
@@ -13,7 +13,7 @@
 LANES = 128
 EPSILON = 1e-06
 AHEAD = 8
-PLAN = {0: ('wsx', 'ra0xc'), 1: ('ro1y', 'ro1xc'), (1, 2): (), 6: ('ra1', 'ro3', 'wsy', 'wsz', 'wsc'), (2, 2): ('ra2',), 10: ('ra3', 'wo1', 'wa0'), 11: ('rb0', 'rb1', 'rb2', 'rb3', 'wo2'), (1, 1): ('ro1z',), (1, 3): ('ro2',), 12: ('wa1', 'wo3'), 14: ('wa2',), 15: ('wa3',), 16: ('wb0', 'wb1'), 17: ('wb2', 'wb3')}
+PLAN = {0: ('ra0xc',), 1: ('ro1y', 'ro1xc', 'wsx'), (1, 2): (), 6: ('ra1', 'ro3', 'wsy', 'wsz', 'wsc'), (2, 2): ('ra2',), 10: ('ra3', 'wo1', 'wa0'), 11: ('rb0', 'rb1', 'rb2', 'rb3', 'wo2'), (1, 1): ('ro1z',), (1, 3): ('ro2',), 12: ('wa1', 'wo3'), 14: ('wa2',), 15: ('wa3',), 16: ('wb0', 'wb1'), 17: ('wb2', 'wb3')}
 MESH = pl.DeviceIdType.MESH
 
 

time: 126 us -> 126 us (level)
  no operation moved by 1% of the time
where the time goes in v5:
time: 126 us
  Pallas kernels  122 us (97%)
  local copies, waits for them, and re-layouts  4.64 us (4%)
    pallas_call x1, Pallas kernels, on_device(): pl.pallas_call(functools.partial(layer_kernel, n_grp, n_seq, capacity, re...  122 us
    unnamed x1, local copies, waits for them, and re-layouts  4.64 us

profile of v5, /device:TPU:25, one launch (start us, length us, event | category | flops | bytes accessed | tf_op | source)
XLA Modules:
  0.0 126.3 jit_solution(10235907049732300142)
XLA Ops:
  0.0 121.7 %shard_map.145 = bf16[256,8192]{1,0:T(8,128)(2,1)} custom-call(bf16[64,1280]{1,0:T(8,128)(2,1)} %patches.1, s32[1,64]{1,0:T(1,128)} %pieces.1, f32[1280]{0:T(1024)} %vit_gain.1, f32[1280]{0:T(1024)} %merge_gain.1, f32[8192]{0:T(1024)} %attn_gain.1, s32[256]{0:T(256)} %image_index.1, s32[16]{0:T(128)} %dest.1, s32[1,4]{1,0:T(1,128)} %doc_lengths.1, ...), custom_call_target="tpu_custom_call" | custom-call | tf_op jit(solution)/shard_map/pallas_call | solution.py:689
  121.7 4.6 %copy.17 = bf16[256,8192]{1,0:T(8,128)(2,1)} copy(bf16[256,8192]{1,0:T(8,128)(2,1)} %shard_map.145) | data formatting | bytes 8388608
